TPU v7x, 32 devices: a whole 2x2x4 slice. The times are simulated.
32 devices in a mesh: gx: 2 (over core), gy: 4 (over y, x), gz: 4 (over z).
Axes of the slice: x: 2, y: 2, z: 4, core: 2. Of those that a mesh axis runs over, the one named last changes fastest.
Arguments:
- raw_weight: float32 [128, 27, 128], P(('gx', 'gy')), may hold values from -6 to 6
- inputs: bfloat16 [16, 64, 64, 128], P('gx', 'gy', 'gz'), may hold values from -6 to 6
- cotangent: bfloat16 [16, 64, 64, 128], P('gx', 'gy', 'gz'), may hold values from -0.099609375 to 0.099609375
Outputs:
- input_grad: bfloat16 [16, 64, 64, 128], P('gx', 'gy', 'gz')
- weight_grad: float32 [128, 27, 128], P(('gx', 'gy'))
All inputs are finite; a program needn't handle non-finite values.
Results may differ from a plain program's by a relative error of at most 0.0049.
Values may be sent and summed in bfloat16 or wider, within the bound.
A program may use at most 64 MiB of HBM per device.

v0:
```python
import jax
import jax.numpy as jnp
from jax import lax
from jax.sharding import PartitionSpec as P

var_eps = 1e-05
norm_eps = 1e-06
clip_norm = 600.0


def with_halo(cells, sides, width):
    for axis, dim in sides:
        count = lax.axis_size(axis)
        ends = count - 1
        head = lax.slice_in_dim(cells, 0, width, axis=dim)
        tail = lax.slice_in_dim(cells, cells.shape[dim] - width, cells.shape[dim], axis=dim)
        cells = jnp.concatenate(
            [
                lax.ppermute(tail, axis, [(i, (i + 1) % count) for i in range(ends)]),
                cells,
                lax.ppermute(head, axis, [((i + 1) % count, i) for i in range(ends)]),
            ],
            axis=dim,
        )
    return cells


def tap_view(padded, tap_a, tap_b, tap_c, extent):
    view = padded[
        2 - tap_a : 2 - tap_a + extent[0],
        2 - tap_b : 2 - tap_b + extent[1],
        2 - tap_c : 2 - tap_c + extent[2],
        :,
    ]
    return view.reshape(-1, view.shape[-1])


def input_rows(padded, extent, block_rows):
    row_count = block_rows.shape[0]
    total = jnp.zeros((extent[0] * extent[1] * extent[2], row_count), jnp.float32)
    for tap_a in range(3):
        for tap_b in range(3):
            for tap_c in range(3):
                tap_index = tap_a * 9 + tap_b * 3 + tap_c
                view = tap_view(padded, tap_a, tap_b, tap_c, extent)
                total = total + lax.dot_general(
                    view,
                    block_rows[:, tap_index, :],
                    (((1,), (1,)), ((), ())),
                    preferred_element_type=jnp.float32,
                )
    return total.astype(jnp.bfloat16).reshape(extent[0], extent[1], extent[2], row_count)


def filter_terms(padded, flat_in, extent):
    pieces = []
    for tap_a in range(3):
        for tap_b in range(3):
            for tap_c in range(3):
                view = tap_view(padded, tap_a, tap_b, tap_c, extent)
                pieces.append(
                    lax.dot_general(
                        flat_in, view, (((0,), (0,)), ((), ())), preferred_element_type=jnp.float32
                    )
                )
    return jnp.stack(pieces, axis=1)


def on_device(raw_weight, inputs, cotangent):
    extent = inputs.shape[:3]
    channels = inputs.shape[3]
    fan_count = channels * raw_weight.shape[1]
    padded = with_halo(cotangent, (("gx", 0), ("gy", 1), ("gz", 2)), 1)
    flat_in = inputs.reshape(-1, channels)
    sum_first, sum_second = lax.psum(
        (jnp.sum(raw_weight, axis=(0, 1)), jnp.sum(raw_weight * raw_weight, axis=(0, 1))),
        ("gx", "gy"),
    )
    mean_out = sum_first / fan_count
    var_out = sum_second / fan_count - mean_out * mean_out
    inv_std = lax.rsqrt(var_out + var_eps)
    std_float = (raw_weight - mean_out) * inv_std
    std_whole = lax.all_gather(std_float.astype(jnp.bfloat16), ("gx", "gy"), axis=0, tiled=True)
    input_grad = input_rows(padded, extent, std_whole)
    local_terms = filter_terms(padded, flat_in, extent)
    column_sum = lax.psum(local_terms, "gz")
    filter_grad = lax.psum_scatter(column_sum, ("gx", "gy"), scatter_dimension=0, tiled=True)
    local_grad = jnp.sum(filter_grad, axis=(0, 1))
    local_cross = jnp.sum(filter_grad * std_float, axis=(0, 1))
    local_square = jnp.sum(filter_grad * filter_grad, axis=(0, 1))
    sum_grad, sum_cross, sum_square = lax.psum(
        (local_grad, local_cross, local_square), ("gx", "gy")
    )
    mean_grad = sum_grad / fan_count
    mean_cross = sum_cross / fan_count
    raw_grad = inv_std * (filter_grad - mean_grad - std_float * mean_cross)
    per_output = sum_square - 2.0 * mean_grad * sum_grad - 2.0 * mean_cross * sum_cross
    per_output = (
        per_output
        + fan_count * mean_grad * mean_grad
        + fan_count * mean_cross * mean_cross * var_out / (var_out + var_eps)
    )
    square_sum = jnp.sum(inv_std * inv_std * per_output)
    scale = jnp.minimum(1.0, clip_norm * lax.rsqrt(square_sum + norm_eps))
    return (input_grad, raw_grad * scale)


def solution(mesh):
    in_specs = (P(("gx", "gy"), None, None), P("gx", "gy", "gz", None), P("gx", "gy", "gz", None))
    out_specs = (P("gx", "gy", "gz", None), P(("gx", "gy"), None, None))
    return jax.shard_map(
        on_device, mesh=mesh, in_specs=in_specs, out_specs=out_specs, check_vma=False
    )
```

profile of v0, /device:TPU:0, one launch (start us, length us, event | category | flops | bytes accessed | tf_op | source)
XLA Modules:
  0.0 215.6 jit_solution(4366381669883090917)
XLA Ops:
  8.2 2.4 %collective-permute-start = (bf16[1,16,16,128]{3,2,1,0:T(8,128)(2,1)S(1)}, bf16[1,16,16,128]{3,2,1,0:T(8,128)(2,1)S(1)}, u32[]{:S(2)}, u32[]{:S(2)}) collective-permute-start(bf16[1,16,16,128]{3,2,1,0:T(8,128)(2,1)S(1)} %get-tuple-element.51), channel_id=1, source_target_pairs={{0,16},{1,17},{2,18},{3,19},{4,20},{5,21},{6,22},{7,23},{8,24},{9,... | collective-permute-start | bytes 196616 | tf_op jit(solution)/shard_map/ppermute | solution.py:19
  10.6 1.3 collective-permute-start.1
  11.9 1.4 constant_dynamic-update-slice_fusion.5
  13.8 1.3 collective-permute-start.3
  15.1 4.8 %collective-permute-start.2 = (bf16[10,1,16,128]{3,2,1,0:T(8,128)(2,1)S(1)}, bf16[10,1,16,128]{3,2,1,0:T(8,128)(2,1)S(1)}, u32[]{:S(2)}, u32[]{:S(2)}) collective-permute-start(bf16[10,1,16,128]{3,2,1,0:T(8,128)(2,1)S(1)} %get-tuple-element.45), channel_id=1, source_target_pairs={{0,4},{4,8},{8,12},{1,5},{5,9},{9,13},{2,6},{6,10},{10,14},{3,7},{... | collective-permute-start | bytes 122888 | tf_op jit(solution)/shard_map/ppermute | solution.py:19
  20.3 1.3 collective-permute-done.2
  21.8 1.3 collective-permute-start.4
  23.1 4.6 %collective-permute-start.5 = (bf16[10,18,1,128]{3,2,1,0:T(2,128)(2,1)S(1)}, bf16[10,18,1,128]{3,2,1,0:T(2,128)(2,1)S(1)}, u32[]{:S(2)}, u32[]{:S(2)}) collective-permute-start(bf16[10,18,1,128]{3,2,1,0:T(2,128)(2,1)S(1)} %get-tuple-element.35), channel_id=1, source_target_pairs={{0,1},{1,2},{2,3},{4,5},{5,6},{6,7},{8,9},{9,10},{10,11},{12,13},{... | collective-permute-start | bytes 138248 | tf_op jit(solution)/shard_map/ppermute | solution.py:19
  28.3 1.5 collective-permute-done.5
  30.6 1.0 fusion.29
  31.6 1.0 fusion.10
  32.6 1.0 fusion.28
  33.5 1.0 fusion.27
  34.5 1.0 fusion.9
  35.5 1.0 fusion.26
  36.5 1.0 fusion.25
  37.4 1.0 fusion.8
  38.4 1.0 fusion.24
  39.4 1.0 fusion.23
  40.4 1.0 fusion.7
  42.3 1.0 fusion.21
  43.3 1.0 fusion.20
  44.3 1.0 fusion.19
  45.3 1.0 fusion.18
  46.3 1.0 fusion.6
  47.2 1.0 fusion.17
  48.2 1.0 fusion.16
  51.1 1.0 fusion.14
  52.1 1.0 fusion.4
  53.1 1.0 fusion.13
  54.1 1.0 fusion.12
  55.0 1.0 fusion.3
  56.0 1.0 fusion.11
  57.0 3.1 %copy.12 = f32[128,27,128]{2,1,0:T(8,128)} copy(f32[128,27,128]{0,2,1:T(8,128)} %fusion.11) | data formatting | bytes 3538944 | tf_op jit(solution)/shard_map/stack | solution.py:66
  60.2 1.0 multiply_reduce_fusion.2
  61.2 16.7 %all-reduce.1 = (f32[128]{0:T(128)S(1)}, f32[128]{0:T(128)S(1)}) all-reduce(f32[128]{0:T(128)S(1)} %get-tuple-element.8, f32[128]{0:T(128)S(1)} %get-tuple-element.7), channel_id=1, replica_groups=mesh['gx'=2,'gy'=4,'gz'=4] {'gx','gy'}, use_global_device_ids=true, to_apply=%region_1.0 | all-reduce | flops 256 | bytes 2048 | tf_op jit(solution)/shard_map/psum | solution.py:75
  77.9 1.9 slice.299
  79.8 1.9 slice.338
  81.7 1.7 fusion.32
  83.4 22.2 %reduce-scatter.2.cloned.1.call-done = f32[16,27,128]{2,1,0:T(8,128)} async-done(((f32[128,27,128]{2,1,0:T(8,128)}), f32[16,27,128]{2,1,0:T(8,128)}) %reduce-scatter.2.cloned.1.call-update) | async-done | bytes 221200 | tf_op jit(solution)/shard_map/reduce_scatter | solution.py:87
  105.6 1.8 copy.13
  107.4 3.7 %fusion.65 = (bf16[8,16,16,128]{3,2,1,0:T(8,128)(2,1)}, bf16[8,16,16,128]{3,2,1,0:T(8,128)(2,1)}, bf16[8,16,16,128]{3,2,1,0:T(8,128)(2,1)}, bf16[8,16,16,128]{3,...) fusion(bf16[10,18,17,128]{3,2,1,0:T(8,128)(2,1)S(1)} %get-tuple, ...), kind=kLoop, calls=%fused_computation.177 | loop fusion | bytes 18874368 | tf_op jit(solution)/shard_map/slice | solution.py:29
  111.1 32.5 %all-reduce.4.cloned.1.call-done = f32[16,27,128]{2,0,1:T(8,128)} async-done(((f32[16,27,128]{2,0,1:T(8,128)}), f32[16,27,128]{2,0,1:T(8,128)}) %all-reduce.4.cloned.1.call-update) | async-done | bytes 221200 | tf_op jit(solution)/shard_map/psum | solution.py:86
  143.6 1.1 multiply_reduce_fusion
  144.8 14.4 %all-reduce = (f32[128]{0:T(128)S(1)}, f32[128]{0:T(128)S(1)}, f32[128]{0:T(128)S(1)}) all-reduce(f32[128]{0:T(128)S(1)} %get-tuple-element.5, f32[128]{0:T(128)S(1)} %get-tuple-element.6, f32[128]{0:T(128)S(1)} %get-tuple-element.4), channel_id=1, replica_groups=mesh['gx'=2,'gy'=4,'gz'=4] {'gx','gy'}, use_global_device_ids=true, to_apply=%region_9.0 | all-reduce | flops 384 | bytes 3072 | tf_op jit(solution)/shard_map/psum | solution.py:91
  160.5 1.8 multiply_multiply_fusion
  162.3 27.9 %all_gather.3 = bf16[128,27,128]{2,0,1:T(8,128)(2,1)S(1)} all-gather(bf16[16,27,128]{2,0,1:T(8,128)(2,1)S(1)} %get-tuple-element.53), channel_id=1, replica_groups=mesh['gx'=2,'gy'=4,'gz'=4] {'gx','gy'}, dimensions={0}, use_global_device_ids=true | all-gather | bytes 995328 | tf_op jit(solution)/shard_map/all_gather | solution.py:83
  207.7 1.1 fusion.2
  (105 shorter events, 24.2 us)
Async XLA Ops:
  7.2 23.5 %copy-start = (bf16[8,16,16,128]{3,2,1,0:T(8,128)(2,1)S(1)}, bf16[8,16,16,128]{3,2,1,0:T(8,128)(2,1)}, u32[]{:S(2)}) copy-start(bf16[8,16,16,128]{3,2,1,0:T(8,128)(2,1)} %param.4) | copy-start | bytes 1572868
  7.2 98.4 %reduce-scatter.2.cloned.1.call-start = ((), (), s32[]{:S(2)}) async-start(), calls=%async_computation.1 | async-start | bytes 2359296 | tf_op jit(solution)/shard_map/reduce_scatter | solution.py:87
  8.2 3.7 %collective-permute-start = (bf16[1,16,16,128]{3,2,1,0:T(8,128)(2,1)S(1)}, bf16[1,16,16,128]{3,2,1,0:T(8,128)(2,1)S(1)}, u32[]{:S(2)}, u32[]{:S(2)}) collective-permute-start(bf16[1,16,16,128]{3,2,1,0:T(8,128)(2,1)S(1)} %get-tuple-element.51), channel_id=1, source_target_pairs={{0,16},{1,17},{2,18},{3,19},{4,20},{5,21},{6,22},{7,23},{8,24},{9,... | collective-permute-start | bytes 196616 | tf_op jit(solution)/shard_map/ppermute | solution.py:19
  10.6 3.1 %collective-permute-start.1 = (bf16[1,16,16,128]{3,2,1,0:T(8,128)(2,1)S(1)}, bf16[1,16,16,128]{3,2,1,0:T(8,128)(2,1)S(1)}, u32[]{:S(2)}, u32[]{:S(2)}) collective-permute-start(bf16[1,16,16,128]{3,2,1,0:T(8,128)(2,1)S(1)} %get-tuple-element.50), channel_id=1, source_target_pairs={{16,0},{17,1},{18,2},{19,3},{20,4},{21,5},{22,6},{23,7},{24,8},{25... | collective-permute-start | bytes 196616 | tf_op jit(solution)/shard_map/ppermute | solution.py:21
  13.3 38.8 %copy-start.29 = (bf16[9,16,16,128]{3,2,1,0:T(8,128)(2,1)}, bf16[9,16,16,128]{3,2,1,0:T(8,128)(2,1)S(1)}, u32[]{:S(2)}) copy-start(bf16[9,16,16,128]{3,2,1,0:T(8,128)(2,1)S(1)} %get-tuple-element.47) | copy-start | bytes 1769476
  13.7 20.8 %copy-start.28 = (bf16[9,16,16,128]{3,2,1,0:T(8,128)(2,1)}, bf16[9,16,16,128]{3,2,1,0:T(8,128)(2,1)S(1)}, u32[]{:S(2)}) copy-start(bf16[9,16,16,128]{3,2,1,0:T(8,128)(2,1)S(1)} %get-tuple-element.56) | copy-start | bytes 1769476
  13.8 6.6 %collective-permute-start.3 = (bf16[10,1,16,128]{3,2,1,0:T(8,128)(2,1)S(1)}, bf16[10,1,16,128]{3,2,1,0:T(8,128)(2,1)S(1)}, u32[]{:S(2)}, u32[]{:S(2)}) collective-permute-start(bf16[10,1,16,128]{3,2,1,0:T(8,128)(2,1)S(1)} %get-tuple-element.46), channel_id=1, source_target_pairs={{4,0},{8,4},{12,8},{5,1},{9,5},{13,9},{6,2},{10,6},{14,10},{7,3},{... | collective-permute-start | bytes 122888 | tf_op jit(solution)/shard_map/ppermute | solution.py:21
  15.1 6.6 %collective-permute-start.2 = (bf16[10,1,16,128]{3,2,1,0:T(8,128)(2,1)S(1)}, bf16[10,1,16,128]{3,2,1,0:T(8,128)(2,1)S(1)}, u32[]{:S(2)}, u32[]{:S(2)}) collective-permute-start(bf16[10,1,16,128]{3,2,1,0:T(8,128)(2,1)S(1)} %get-tuple-element.45), channel_id=1, source_target_pairs={{0,4},{4,8},{8,12},{1,5},{5,9},{9,13},{2,6},{6,10},{10,14},{3,7},{... | collective-permute-start | bytes 122888 | tf_op jit(solution)/shard_map/ppermute | solution.py:19
  21.8 6.5 %collective-permute-start.4 = (bf16[10,18,1,128]{3,2,1,0:T(2,128)(2,1)S(1)}, bf16[10,18,1,128]{3,2,1,0:T(2,128)(2,1)S(1)}, u32[]{:S(2)}, u32[]{:S(2)}) collective-permute-start(bf16[10,18,1,128]{3,2,1,0:T(2,128)(2,1)S(1)} %get-tuple-element.34), channel_id=1, source_target_pairs={{1,0},{2,1},{3,2},{5,4},{6,5},{7,6},{9,8},{10,9},{11,10},{13,12},{... | collective-permute-start | bytes 138248 | tf_op jit(solution)/shard_map/ppermute | solution.py:21
  23.1 6.7 %collective-permute-start.5 = (bf16[10,18,1,128]{3,2,1,0:T(2,128)(2,1)S(1)}, bf16[10,18,1,128]{3,2,1,0:T(2,128)(2,1)S(1)}, u32[]{:S(2)}, u32[]{:S(2)}) collective-permute-start(bf16[10,18,1,128]{3,2,1,0:T(2,128)(2,1)S(1)} %get-tuple-element.35), channel_id=1, source_target_pairs={{0,1},{1,2},{2,3},{4,5},{5,6},{6,7},{8,9},{9,10},{10,11},{12,13},{... | collective-permute-start | bytes 138248 | tf_op jit(solution)/shard_map/ppermute | solution.py:19
  42.3 1.0 copy-start.1
  60.2 83.5 %all-reduce.4.cloned.1.call-start = ((), (), s32[]{:S(2)}) async-start(), calls=%async_computation.2 | async-start | bytes 442368 | tf_op jit(solution)/shard_map/psum | solution.py:86
  144.8 45.7 %copy-start.22 = (bf16[8,16,16,128]{3,2,1,0:T(8,128)(2,1)S(1)}, bf16[8,16,16,128]{3,2,1,0:T(8,128)(2,1)}, u32[]{:S(2)}) copy-start(bf16[8,16,16,128]{3,2,1,0:T(8,128)(2,1)} %get-tuple-element.43) | copy-start | bytes 1572868
  190.1 1.0 copy-start.20
  190.4 1.1 copy-start.19
  191.5 1.1 copy-start.18
  191.8 1.1 copy-start.3
  192.9 1.0 copy-start.17
  193.2 1.1 copy-start.27
  194.2 1.1 copy-start.16
  194.6 1.1 copy-start.15
  195.6 1.1 copy-start.26
  196.0 1.1 copy-start.14
  197.0 1.1 copy-start.13
  197.4 1.1 copy-start.2
  198.3 1.1 copy-start.12
  198.7 1.1 copy-start.11
  199.7 1.1 copy-start.25
  200.1 1.1 copy-start.10
  201.1 1.1 copy-start.9
  201.5 1.1 copy-start.24
  202.4 1.1 copy-start.8
  202.9 1.1 copy-start.7
  203.8 1.1 copy-start.21
  204.3 1.1 copy-start.6
  205.2 1.1 copy-start.5
  205.6 1.1 copy-start.23
  206.6 1.1 copy-start.4
Sparse Core Ops, SparseCore 0:
  60.3 45.2 reduce-scatter.1
  108.5 35.0 all-reduce.3
where the time goes:
time: 217 us; the launch traced here: 216 us
  waiting for transfers between devices  59 us (27%)
  blocking collectives  58.9 us (27%)
  matrix products  35 us (16%)
  local copies, waits for them, and re-layouts  24.4 us (11%)
  starting transfers between devices  15.8 us (7%)
  between operations  15.2 us (7%)
  other arithmetic  7.2 us (3%)
    psum x1, waiting for transfers between devices, on_device(): column_sum = lax.psum(local_terms, 'gz')  32.5 us
    all_gather x1, blocking collectives, on_device(): lax.all_gather(std_float.astype(jnp.bfloat16), ('gx', 'gy'), axis=0, tile...  27.9 us
    dot_general x27, matrix products, filter_terms(): lax.dot_general(flat_in, view, (((0,), (0,)), ((), ())), preferred_elemen...  26.3 us
    reduce_scatter x1, waiting for transfers between devices, on_device(): lax.psum_scatter(column_sum, ('gx', 'gy'), scatter_dimension=0, tiled=True)  22.2 us
    psum x1, blocking collectives, on_device(): lax.psum((jnp.sum(raw_weight, axis=(0, 1)), jnp.sum(raw_weight * raw_weig...  16.7 us
    psum x1, blocking collectives, on_device(): lax.psum((local_grad, local_cross, local_square), ('gx', 'gy'))  14.4 us
    ppermute x3, starting transfers between devices, with_halo(): lax.ppermute(tail, axis, [(i, (i + 1) % count) for i in range(ends)])  11.8 us
    unnamed x61, local copies, waits for them, and re-layouts  9.64 us
  transfers between devices with their start and end apart: 8, of which 7 were waited for; matrix products, arithmetic and copies ran while one was open for 5% of the time, Pallas kernels for 0%

commit v1 on v0

--- a/solution.py
+++ b/solution.py
@@ -83,7 +83,11 @@
     std_whole = lax.all_gather(std_float.astype(jnp.bfloat16), ("gx", "gy"), axis=0, tiled=True)
     input_grad = input_rows(padded, extent, std_whole)
     local_terms = filter_terms(padded, flat_in, extent)
-    column_sum = lax.psum(local_terms, "gz")
+    column_sum = local_terms
+    for hop in (1, 2):
+        column_sum = column_sum + lax.ppermute(
+            column_sum, "gz", [(dev, dev ^ hop) for dev in range(4)]
+        )
     filter_grad = lax.psum_scatter(column_sum, ("gx", "gy"), scatter_dimension=0, tiled=True)
     local_grad = jnp.sum(filter_grad, axis=(0, 1))
     local_cross = jnp.sum(filter_grad * std_float, axis=(0, 1))

time: 217 us -> 280 us (1.29)
  waiting for transfers between devices: 59 us -> 133 us
  matrix products: 35 us -> 18.1 us
  starting transfers between devices: 15.8 us -> 21.2 us
  other arithmetic: 7.2 us -> 10.1 us
    ppermute x0 -> x2, waiting for transfers between devices: none -> 112 us  [on_device(): lax.ppermute(column_sum, 'gz', [(dev, dev ^ hop) for dev in range(4)])]
    psum x1 -> x0, waiting for transfers between devices: 32.5 us -> none  [on_device(): column_sum = lax.psum(local_terms, 'gz')]
    dot_general x27, matrix products: 26.3 us -> 9.36 us  [filter_terms(): lax.dot_general(flat_in, view, (((0,), (0,)), ((), ())), preferred_elemen...]
    ppermute x0 -> x2, starting transfers between devices: none -> 5.44 us  [on_device(): lax.ppermute(column_sum, 'gz', [(dev, dev ^ hop) for dev in range(4)])]
    reduce_scatter x1, waiting for transfers between devices: 22.2 us -> 17.5 us  [on_device(): lax.psum_scatter(column_sum, ('gx', 'gy'), scatter_dimension=0, tiled=True)]
    another operation x1 -> x0, local copies, waits for them, and re-layouts: 3.15 us -> none  [filter_terms(): return jnp.stack(pieces, axis=1)]
    add x0 -> x1, local copies, waits for them, and re-layouts: none -> 3.09 us  [on_device(): column_sum + lax.ppermute(column_sum, 'gz', [(dev, dev ^ hop) for dev in...]
  transfers between devices with their start and end apart: 8 -> 9, of which waited for: 7 -> 8; matrix products, arithmetic and copies ran while one was open for 5% -> 4% of each run, Pallas kernels for 0% -> 0%
where the time goes in v1:
time: 280 us; the launch traced here: 279 us
  waiting for transfers between devices  133 us (48%)
  blocking collectives  57.7 us (21%)
  local copies, waits for them, and re-layouts  23.2 us (8%)
  starting transfers between devices  21.2 us (8%)
  matrix products  18.1 us (6%)
  between operations  15.4 us (6%)
  other arithmetic  10.1 us (4%)
    ppermute x2, waiting for transfers between devices, on_device(): lax.ppermute(column_sum, 'gz', [(dev, dev ^ hop) for dev in range(4)])  112 us
    all_gather x1, blocking collectives, on_device(): lax.all_gather(std_float.astype(jnp.bfloat16), ('gx', 'gy'), axis=0, tile...  27.8 us
    reduce_scatter x1, waiting for transfers between devices, on_device(): lax.psum_scatter(column_sum, ('gx', 'gy'), scatter_dimension=0, tiled=True)  17.5 us
    psum x1, blocking collectives, on_device(): lax.psum((jnp.sum(raw_weight, axis=(0, 1)), jnp.sum(raw_weight * raw_weig...  15.5 us
    psum x1, blocking collectives, on_device(): lax.psum((local_grad, local_cross, local_square), ('gx', 'gy'))  14.4 us
    ppermute x3, starting transfers between devices, with_halo(): lax.ppermute(tail, axis, [(i, (i + 1) % count) for i in range(ends)])  11.8 us
    unnamed x61, local copies, waits for them, and re-layouts  10.2 us
    dot_general x27, matrix products, filter_terms(): lax.dot_general(flat_in, view, (((0,), (0,)), ((), ())), preferred_elemen...  9.36 us
  transfers between devices with their start and end apart: 9, of which 8 were waited for; matrix products, arithmetic and copies ran while one was open for 4% of the time, Pallas kernels for 0%

profile of v1, /device:TPU:0, one launch (start us, length us, event | category | flops | bytes accessed | tf_op | source)
XLA Modules:
  0.0 279.0 jit_solution(276892713439819950)
XLA Ops:
  7.2 0.9 fusion.68
  8.2 2.4 collective-permute-start
  10.6 1.3 collective-permute-start.1
  11.9 1.4 constant_dynamic-update-slice_fusion.5
  13.3 0.4 collective-permute-done.1
  13.8 1.3 collective-permute-start.3
  15.1 4.8 %collective-permute-start.2 = (bf16[10,1,16,128]{3,2,1,0:T(8,128)(2,1)S(1)}, bf16[10,1,16,128]{3,2,1,0:T(8,128)(2,1)S(1)}, u32[]{:S(2)}, u32[]{:S(2)}) collective-permute-start(bf16[10,1,16,128]{3,2,1,0:T(8,128)(2,1)S(1)} %get-tuple-element.44), channel_id=1, source_target_pairs={{0,4},{4,8},{8,12},{1,5},{5,9},{9,13},{2,6},{6,10},{10,14},{3,7},{... | collective-permute-start | bytes 122888 | tf_op jit(solution)/shard_map/ppermute | solution.py:19
  19.9 0.4 collective-permute-done.3
  20.3 1.3 collective-permute-done.2
  21.8 1.3 collective-permute-start.4
  23.1 4.6 %collective-permute-start.5 = (bf16[10,18,1,128]{3,2,1,0:T(2,128)(2,1)S(1)}, bf16[10,18,1,128]{3,2,1,0:T(2,128)(2,1)S(1)}, u32[]{:S(2)}, u32[]{:S(2)}) collective-permute-start(bf16[10,18,1,128]{3,2,1,0:T(2,128)(2,1)S(1)} %get-tuple-element.34), channel_id=1, source_target_pairs={{0,1},{1,2},{2,3},{4,5},{5,6},{6,7},{8,9},{9,10},{10,11},{12,13},{... | collective-permute-start | bytes 138248 | tf_op jit(solution)/shard_map/ppermute | solution.py:19
  27.7 0.6 collective-permute-done.4
  28.3 1.5 collective-permute-done.5
  29.8 0.8 pad_maximum_fusion.2
  35.2 0.7 copy-done.1
  40.9 2.5 collective-permute-start.6
  43.3 37.2 %collective-permute-done.6 = f32[128,27,128]{0,2,1:T(8,128)S(1)} collective-permute-done((f32[128,27,128]{0,2,1:T(8,128)S(1)}, f32[128,27,128]{0,2,1:T(8,128)S(1)}, u32[]{:S(2)}, u32[]{:S(2)}) %collective-permute-start.6) | collective-permute-done | bytes 1769504 | tf_op jit(solution)/shard_map/ppermute | solution.py:88
  80.8 3.0 %collective-permute-start.7 = (f32[128,27,128]{0,2,1:T(8,128)S(1)}, f32[128,27,128]{0,2,1:T(8,128)S(1)}, u32[]{:S(2)}, u32[]{:S(2)}) collective-permute-start(f32[128,27,128]{0,2,1:T(8,128)S(1)} %add.136), channel_id=1, source_target_pairs={{0,2},{1,3},{2,0},{3,1},{4,6},{5,7},{6,4},{7,5},{8,10},{9,11},{10,... | collective-permute-start | bytes 5308424 | tf_op jit(solution)/shard_map/ppermute | solution.py:88
  83.8 74.3 %collective-permute-done.7 = f32[128,27,128]{0,2,1:T(8,128)S(1)} collective-permute-done((f32[128,27,128]{0,2,1:T(8,128)S(1)}, f32[128,27,128]{0,2,1:T(8,128)S(1)}, u32[]{:S(2)}, u32[]{:S(2)}) %collective-permute-start.7) | collective-permute-done | bytes 1769504 | tf_op jit(solution)/shard_map/ppermute | solution.py:88
  158.1 1.4 add.137
  159.5 3.1 %copy.12 = f32[128,27,128]{2,1,0:T(8,128)} copy(f32[128,27,128]{0,2,1:T(8,128)} %add.137) | data formatting | bytes 3538944 | tf_op jit(solution)/shard_map/add | solution.py:88
  162.6 1.0 multiply_reduce_fusion.2
  163.7 15.5 %all-reduce.1 = (f32[128]{0:T(128)S(1)}, f32[128]{0:T(128)S(1)}) all-reduce(f32[128]{0:T(128)S(1)} %get-tuple-element.7, f32[128]{0:T(128)S(1)} %get-tuple-element.6), channel_id=1, replica_groups=mesh['gx'=2,'gy'=4,'gz'=4] {'gx','gy'}, use_global_device_ids=true, to_apply=%region_1.0 | all-reduce | flops 256 | bytes 2048 | tf_op jit(solution)/shard_map/psum | solution.py:75
  179.2 1.9 slice.299
  181.1 1.9 slice.338
  183.0 1.8 fusion.32
  184.7 3.7 %fusion.65 = (bf16[8,16,16,128]{3,2,1,0:T(8,128)(2,1)}, bf16[8,16,16,128]{3,2,1,0:T(8,128)(2,1)}, bf16[8,16,16,128]{3,2,1,0:T(8,128)(2,1)}, bf16[8,16,16,128]{3,...) fusion(bf16[10,18,17,128]{3,2,1,0:T(8,128)(2,1)S(1)} %get-tuple, ...), kind=kLoop, calls=%fused_computation.177 | loop fusion | bytes 18874368 | tf_op jit(solution)/shard_map/slice | solution.py:29
  188.5 17.5 %reduce-scatter.2.cloned.1.call-done = f32[16,27,128]{2,1,0:T(8,128)} async-done(((f32[128,27,128]{2,1,0:T(8,128)}), f32[16,27,128]{2,1,0:T(8,128)}) %reduce-scatter.2.cloned.1.call-update) | async-done | bytes 221200 | tf_op jit(solution)/shard_map/reduce_scatter | solution.py:91
  205.9 1.0 multiply_reduce_fusion
  206.9 1.2 multiply_reduce_fusion.1
  208.1 14.4 %all-reduce = (f32[128]{0:T(128)S(1)}, f32[128]{0:T(128)S(1)}, f32[128]{0:T(128)S(1)}) all-reduce(f32[128]{0:T(128)S(1)} %multiply_reduce_fusion.1, f32[128]{0:T(128)S(1)} %get-tuple-element.5, f32[128]{0:T(128)S(1)} %get-tuple-element.4), channel_id=1, replica_groups=mesh['gx'=2,'gy'=4,'gz'=4] {'gx','gy'}, use_global_device_ids=true, to_apply=%region_8.0 | all-reduce | flops 384 | bytes 3072 | tf_op jit(solution)/shard_map/psum | solution.py:95
  222.5 0.6 broadcast_multiply_fusion.1
  223.8 1.9 multiply_multiply_fusion
  225.7 27.8 %all_gather.3 = bf16[128,27,128]{2,0,1:T(8,128)(2,1)S(1)} all-gather(bf16[16,27,128]{2,0,1:T(8,128)(2,1)S(1)} %get-tuple-element.52), channel_id=1, replica_groups=mesh['gx'=2,'gy'=4,'gz'=4] {'gx','gy'}, dimensions={0}, use_global_device_ids=true | all-gather | bytes 995328 | tf_op jit(solution)/shard_map/all_gather | solution.py:83
  254.1 0.4 copy-done.20
  255.2 0.7 copy-done.18
  256.6 0.7 copy-done.17
  258.0 0.7 copy-done.16
  259.3 0.7 copy-done.26
  260.7 0.7 copy-done.13
  262.1 0.6 copy-done.12
  263.5 0.6 copy-done.25
  264.9 0.6 copy-done.9
  266.2 0.6 copy-done.8
  267.6 0.6 copy-done.21
  269.0 0.6 copy-done.5
  270.4 0.6 copy-done.4
  271.0 1.1 fusion.2
  (108 shorter events, 18.7 us)
Async XLA Ops:
  7.2 23.5 %copy-start = (bf16[8,16,16,128]{3,2,1,0:T(8,128)(2,1)S(1)}, bf16[8,16,16,128]{3,2,1,0:T(8,128)(2,1)}, u32[]{:S(2)}) copy-start(bf16[8,16,16,128]{3,2,1,0:T(8,128)(2,1)} %param.4) | copy-start | bytes 1572868
  7.2 198.7 %reduce-scatter.2.cloned.1.call-start = ((), (), s32[]{:S(2)}) async-start(), calls=%async_computation.1 | async-start | bytes 2359296 | tf_op jit(solution)/shard_map/reduce_scatter | solution.py:91
  8.2 3.7 %collective-permute-start = (bf16[1,16,16,128]{3,2,1,0:T(8,128)(2,1)S(1)}, bf16[1,16,16,128]{3,2,1,0:T(8,128)(2,1)S(1)}, u32[]{:S(2)}, u32[]{:S(2)}) collective-permute-start(bf16[1,16,16,128]{3,2,1,0:T(8,128)(2,1)S(1)} %get-tuple-element.50), channel_id=1, source_target_pairs={{0,16},{1,17},{2,18},{3,19},{4,20},{5,21},{6,22},{7,23},{8,24},{9,... | collective-permute-start | bytes 196616 | tf_op jit(solution)/shard_map/ppermute | solution.py:19
  10.6 3.1 %collective-permute-start.1 = (bf16[1,16,16,128]{3,2,1,0:T(8,128)(2,1)S(1)}, bf16[1,16,16,128]{3,2,1,0:T(8,128)(2,1)S(1)}, u32[]{:S(2)}, u32[]{:S(2)}) collective-permute-start(bf16[1,16,16,128]{3,2,1,0:T(8,128)(2,1)S(1)} %get-tuple-element.49), channel_id=1, source_target_pairs={{16,0},{17,1},{18,2},{19,3},{20,4},{21,5},{22,6},{23,7},{24,8},{25... | collective-permute-start | bytes 196616 | tf_op jit(solution)/shard_map/ppermute | solution.py:21
  13.3 25.8 %copy-start.29 = (bf16[9,16,16,128]{3,2,1,0:T(8,128)(2,1)}, bf16[9,16,16,128]{3,2,1,0:T(8,128)(2,1)S(1)}, u32[]{:S(2)}) copy-start(bf16[9,16,16,128]{3,2,1,0:T(8,128)(2,1)S(1)} %get-tuple-element.46) | copy-start | bytes 1769476
  13.7 18.3 %copy-start.28 = (bf16[9,16,16,128]{3,2,1,0:T(8,128)(2,1)}, bf16[9,16,16,128]{3,2,1,0:T(8,128)(2,1)S(1)}, u32[]{:S(2)}) copy-start(bf16[9,16,16,128]{3,2,1,0:T(8,128)(2,1)S(1)} %get-tuple-element.55) | copy-start | bytes 1769476
  13.8 6.6 %collective-permute-start.3 = (bf16[10,1,16,128]{3,2,1,0:T(8,128)(2,1)S(1)}, bf16[10,1,16,128]{3,2,1,0:T(8,128)(2,1)S(1)}, u32[]{:S(2)}, u32[]{:S(2)}) collective-permute-start(bf16[10,1,16,128]{3,2,1,0:T(8,128)(2,1)S(1)} %get-tuple-element.45), channel_id=1, source_target_pairs={{4,0},{8,4},{12,8},{5,1},{9,5},{13,9},{6,2},{10,6},{14,10},{7,3},{... | collective-permute-start | bytes 122888 | tf_op jit(solution)/shard_map/ppermute | solution.py:21
  15.1 6.6 %collective-permute-start.2 = (bf16[10,1,16,128]{3,2,1,0:T(8,128)(2,1)S(1)}, bf16[10,1,16,128]{3,2,1,0:T(8,128)(2,1)S(1)}, u32[]{:S(2)}, u32[]{:S(2)}) collective-permute-start(bf16[10,1,16,128]{3,2,1,0:T(8,128)(2,1)S(1)} %get-tuple-element.44), channel_id=1, source_target_pairs={{0,4},{4,8},{8,12},{1,5},{5,9},{9,13},{2,6},{6,10},{10,14},{3,7},{... | collective-permute-start | bytes 122888 | tf_op jit(solution)/shard_map/ppermute | solution.py:19
  21.8 6.5 %collective-permute-start.4 = (bf16[10,18,1,128]{3,2,1,0:T(2,128)(2,1)S(1)}, bf16[10,18,1,128]{3,2,1,0:T(2,128)(2,1)S(1)}, u32[]{:S(2)}, u32[]{:S(2)}) collective-permute-start(bf16[10,18,1,128]{3,2,1,0:T(2,128)(2,1)S(1)} %get-tuple-element.33), channel_id=1, source_target_pairs={{1,0},{2,1},{3,2},{5,4},{6,5},{7,6},{9,8},{10,9},{11,10},{13,12},{... | collective-permute-start | bytes 138248 | tf_op jit(solution)/shard_map/ppermute | solution.py:21
  23.1 6.7 %collective-permute-start.5 = (bf16[10,18,1,128]{3,2,1,0:T(2,128)(2,1)S(1)}, bf16[10,18,1,128]{3,2,1,0:T(2,128)(2,1)S(1)}, u32[]{:S(2)}, u32[]{:S(2)}) collective-permute-start(bf16[10,18,1,128]{3,2,1,0:T(2,128)(2,1)S(1)} %get-tuple-element.34), channel_id=1, source_target_pairs={{0,1},{1,2},{2,3},{4,5},{5,6},{6,7},{8,9},{9,10},{10,11},{12,13},{... | collective-permute-start | bytes 138248 | tf_op jit(solution)/shard_map/ppermute | solution.py:19
  34.9 1.0 copy-start.1
  40.9 39.7 %collective-permute-start.6 = (f32[128,27,128]{0,2,1:T(8,128)S(1)}, f32[128,27,128]{0,2,1:T(8,128)S(1)}, u32[]{:S(2)}, u32[]{:S(2)}) collective-permute-start(f32[128,27,128]{0,2,1:T(8,128)S(1)} %fusion.11), channel_id=1, source_target_pairs={{0,1},{1,0},{2,3},{3,2},{4,5},{5,4},{6,7},{7,6},{8,9},{9,8},{10,11... | collective-permute-start | bytes 5308424 | tf_op jit(solution)/shard_map/ppermute | solution.py:88
  80.8 77.3 %collective-permute-start.7 = (f32[128,27,128]{0,2,1:T(8,128)S(1)}, f32[128,27,128]{0,2,1:T(8,128)S(1)}, u32[]{:S(2)}, u32[]{:S(2)}) collective-permute-start(f32[128,27,128]{0,2,1:T(8,128)S(1)} %add.136), channel_id=1, source_target_pairs={{0,2},{1,3},{2,0},{3,1},{4,6},{5,7},{6,4},{7,5},{8,10},{9,11},{10,... | collective-permute-start | bytes 5308424 | tf_op jit(solution)/shard_map/ppermute | solution.py:88
  208.1 45.7 %copy-start.22 = (bf16[8,16,16,128]{3,2,1,0:T(8,128)(2,1)S(1)}, bf16[8,16,16,128]{3,2,1,0:T(8,128)(2,1)}, u32[]{:S(2)}) copy-start(bf16[8,16,16,128]{3,2,1,0:T(8,128)(2,1)} %get-tuple-element.42) | copy-start | bytes 1572868
  253.5 1.0 copy-start.20
  253.8 1.1 copy-start.19
  254.8 1.1 copy-start.18
  255.2 1.1 copy-start.3
  256.3 1.0 copy-start.17
  256.6 1.1 copy-start.27
  257.6 1.1 copy-start.16
  258.0 1.1 copy-start.15
  259.0 1.1 copy-start.26
  259.3 1.1 copy-start.14
  260.3 1.1 copy-start.13
  260.7 1.1 copy-start.2
  261.7 1.1 copy-start.12
  262.1 1.1 copy-start.11
  263.1 1.1 copy-start.25
  263.5 1.1 copy-start.10
  264.4 1.1 copy-start.9
  264.9 1.1 copy-start.24
  265.8 1.1 copy-start.8
  266.2 1.1 copy-start.7
  267.2 1.1 copy-start.21
  267.6 1.1 copy-start.6
  268.6 1.1 copy-start.5
  269.0 1.1 copy-start.23
  269.9 1.1 copy-start.4
Sparse Core Ops, SparseCore 0:
  162.8 43.0 reduce-scatter.1
